TPU v7x, 32 devices: a whole 2x2x4 slice. The times are simulated.
32 devices in a mesh: grp: 2 (over y), row: 4 (over x, core), sub: 4 (over z).
Axes of the slice: x: 2, y: 2, z: 4, core: 2. Of those that a mesh axis runs over, the one named last changes fastest.
Arguments:
- residual_in: float32 [4, 2048, 2048], P('grp', ('row', 'sub')), parts along dimension 0, may hold values from -100 to 100
- direction: float32 [4, 2048, 2048], P('grp', ('row', 'sub')), parts along dimension 0, may hold values from -100 to 100
- spectrum: float32 [8192, 4096], P('grp', ('row', 'sub')), parts along dimension 0, may hold values from 0.0999 to 10.001, as said below
- noise_var: float32 [2], P('grp'), parts along dimension 0, may hold values from 0.5 to 2
Outputs:
- residual_out: float32 [4, 2048, 2048], P('grp', ('row', 'sub')), parts along dimension 0
- direction_out: float32 [4, 2048, 2048], P('grp', ('row', 'sub')), parts along dimension 0
- step_size: float32 [4], P('grp'), parts along dimension 0
There are 2 independent parts, one for each index of `grp`. A program takes and returns all parts, laid end to end along the dimension named above; each array names one. Nothing has to cross between parts.
Inputs may be any that keep to these rules, and one draw needn't show every extreme that they name: spectrum[k, l] = spectrum[(4096 - k) % 4096, (4096 - l) % 4096] for all k, l.
All inputs are finite; a program needn't handle non-finite values.
Results may differ from a plain program's by a relative error of at most 0.00005.
Values sent between devices are 32-bit elements; how exact they have to be, the bound alone decides.
A program may use at most 128 MiB of HBM per device.

v0:
```python
import functools
import math

import jax
import jax.numpy as jnp
import numpy as np
from jax import lax
from jax.experimental import pallas as pl
from jax.experimental.pallas import tpu as pltpu
from jax.sharding import PartitionSpec as P

LANES = 128
TINY = 1e-06
CHUNKS = 4
MESH = pl.DeviceIdType.MESH
GRANT = 60 * 1024 * 1024


def unit(turns, modulus, orient):
    angle = orient * 2.0 * np.pi * (np.asarray(turns) % modulus) / modulus
    return np.cos(angle), np.sin(angle)


def halves(table):
    table = np.asarray(table, np.float32)
    hi = table.astype(jnp.bfloat16)
    lo = (table - hi.astype(np.float32)).astype(jnp.bfloat16)
    return jnp.asarray(np.stack([hi, lo]))


def complex_block(cos_part, sin_part):
    return np.stack(
        [np.stack([cos_part, sin_part], 1), np.stack([-sin_part, cos_part], 1)], 0
    )


def split(x):
    hi = x.astype(jnp.bfloat16)
    return hi, (x - hi.astype(jnp.float32)).astype(jnp.bfloat16)


def dot(a, b):
    return jnp.dot(a, b, preferred_element_type=jnp.float32)


def dot_right(x, table_ref):
    hi, lo = split(x)
    return dot(hi, table_ref[0]) + (dot(lo, table_ref[0]) + dot(hi, table_ref[1]))


def dot_left(table_ref, x):
    hi, lo = split(x)
    return dot(table_ref[0], hi) + (dot(table_ref[0], lo) + dot(table_ref[1], hi))


def turn(z, k, n, orient):
    k = k % n
    re, im = z
    if k == 0:
        return z
    if 2 * k == n:
        return -re, -im
    if 4 * k == n or 4 * k == 3 * n:
        sign = orient if 4 * k == n else -orient
        return (-im, re) if sign > 0 else (im, -re)
    c = math.cos(2 * math.pi * k / n)
    s = orient * math.sin(2 * math.pi * k / n)
    return re * c - im * s, re * s + im * c


def add(u, v):
    return u[0] + v[0], u[1] + v[1]


def sub(u, v):
    return u[0] - v[0], u[1] - v[1]


def butterflies(xs, orient):
    n = len(xs)
    if n == 1:
        return xs
    even = butterflies(xs[0::2], orient)
    odd = butterflies(xs[1::2], orient)
    odd = [turn(z, k, n, orient) for k, z in enumerate(odd)]
    return [add(e, o) for e, o in zip(even, odd)] + [sub(e, o) for e, o in zip(even, odd)]


def padded_forward(xs):
    n = len(xs)
    even = butterflies(xs, -1)
    odd = butterflies([turn(z, a, 2 * n, -1) for a, z in enumerate(xs)], -1)
    return [even[i // 2] if i % 2 == 0 else odd[i // 2] for i in range(2 * n)]


def cut_inverse(zs):
    n = len(zs) // 2
    even = butterflies(zs[0::2], 1)
    odd = butterflies(zs[1::2], 1)
    return [add(even[a], turn(odd[a], a, 2 * n, 1)) for a in range(n)]


def rotate(re, im, c, s):
    return re * c - im * s, re * s + im * c


def row_kernel(low, groups, dir_ref, table_ref, cos_ref, sin_ref, *rest):
    outs, work, turned = rest[:-2], rest[-2], rest[-1]
    half = low // 2
    rows = dir_ref.shape[1]
    for c in range(2):
        for a in range(half):
            turned[a, c] = dir_ref[c, :, a * LANES : (a + 1) * LANES].T

    def spread(t, carry):
        at = pl.ds(pl.multiple_of(t * 8, 8), 8)
        xs = [(turned[a, 0, at, :], turned[a, 1, at, :]) for a in range(half)]
        cos_rows, sin_rows = cos_ref[at, :], sin_ref[at, :]
        for m, (re, im) in enumerate(padded_forward(xs)):
            re, im = rotate(re, im, cos_rows[:, m : m + 1], sin_rows[:, m : m + 1])
            work[m, 0, at, :] = re
            work[m, 1, at, :] = im
        return carry

    lax.fori_loop(0, LANES // 8, spread, 0)
    per_chunk = low // len(outs)
    for i, out in enumerate(outs):

        def column(m, carry):
            got = dot_left(table_ref, work[i * per_chunk + m].reshape(2 * LANES, rows))
            size = 2 * LANES // groups
            for j in range(groups):
                out[j, m] = got[j * size : (j + 1) * size]
            return carry

        lax.fori_loop(0, per_chunk, column, 0)


def column_kernel(low, per, x_ref, w_ref, fwd_ref, inv_ref, cos_ref, sin_ref, out_ref, work):
    half = low // 2
    count = x_ref.shape[1]

    def spread(m, carry):
        xs = [(x_ref[a, m, :per], x_ref[a, m, per:]) for a in range(half)]
        for k, (re, im) in enumerate(padded_forward(xs)):
            re, im = rotate(re, im, cos_ref[k : k + 1, :], sin_ref[k : k + 1, :])
            work[k, m, :, :LANES] = re
            work[k, m, :, LANES:] = im
        return carry

    lax.fori_loop(0, count, spread, 0)

    def filtered(k, carry):
        spectral = dot_right(work[k].reshape(count * per, 2 * LANES), fwd_ref)
        weights = w_ref[k].reshape(count * per, LANES)
        spectral = spectral * jnp.concatenate([weights, weights], axis=1)
        got = dot_right(spectral, inv_ref)
        cos_row, sin_row = cos_ref[pl.ds(k, 1), :], sin_ref[pl.ds(k, 1), :]
        re, im = rotate(got[:, :LANES], got[:, LANES:], cos_row, -sin_row)
        work[k, :, :, :LANES] = re.reshape(count, per, LANES)
        work[k, :, :, LANES:] = im.reshape(count, per, LANES)
        return carry

    lax.fori_loop(0, low, filtered, 0)

    def gather(m, carry):
        zs = [(work[k, m, :, :LANES], work[k, m, :, LANES:]) for k in range(low)]
        for a, (re, im) in enumerate(cut_inverse(zs)):
            out_ref[a, m, :per] = re
            out_ref[a, m, per:] = im
        return carry

    lax.fori_loop(0, count, gather, 0)


def image_kernel(low, groups, chunks, *refs):
    ins = refs[:chunks]
    dir_ref, res_ref, noise_ref, table_ref, cos_ref, sin_ref = refs[chunks : chunks + 6]
    image_ref, sums_ref, work, applied = refs[chunks + 6 :]
    half = low // 2
    rows = dir_ref.shape[1]
    per_chunk = low // chunks
    for i, x_ref in enumerate(ins):

        def column(m, carry):
            parts = [x_ref[j, m] for j in range(groups)]
            got = dot_left(table_ref, parts[0] if groups == 1 else jnp.concatenate(parts, axis=0))
            work[i * per_chunk + m] = got.reshape(2, LANES, rows)
            return carry

        lax.fori_loop(0, per_chunk, column, 0)

    def gather(t, carry):
        at = pl.ds(pl.multiple_of(t * 8, 8), 8)
        cos_rows, sin_rows = cos_ref[at, :], sin_ref[at, :]
        zs = []
        for m in range(low):
            zs.append(
                rotate(work[m, 0, at, :], work[m, 1, at, :], cos_rows[:, m : m + 1], -sin_rows[:, m : m + 1])
            )
        for a, (re, im) in enumerate(cut_inverse(zs)):
            applied[a, 0, at, :] = re
            applied[a, 1, at, :] = im
        return carry

    lax.fori_loop(0, LANES // 8, gather, 0)
    noise = noise_ref[0]
    for c in range(2):
        totals = [jnp.zeros((rows, LANES), jnp.float32)] * 4
        for a in range(half):
            cols = slice(a * LANES, (a + 1) * LANES)
            d, r = dir_ref[c, :, cols], res_ref[c, :, cols]
            image = applied[a, c].T + noise * d
            image_ref[c, :, cols] = image
            for s, term in enumerate((r * r, d * image, r * image, image * image)):
                totals[s] = totals[s] + term
        for s in range(4):
            sums_ref[4 * c + s : 4 * c + s + 1, :] = jnp.sum(totals[s], axis=0, keepdims=True)


def update_kernel(n_row, n_sub, sums_ref, image_ref, dir_ref, res_ref, r_out, d_out, s_out, held, send_sem, recv_sem):
    n = n_row * n_sub
    me = lax.axis_index("row") * n_sub + lax.axis_index("sub")

    def place(o):
        peer = lax.rem(me + o, n)
        return {"row": peer // n_sub, "sub": lax.rem(peer, n_sub)}

    barrier = pltpu.get_barrier_semaphore()

    def greet(o, carry):
        pl.semaphore_signal(barrier, inc=1, device_id=place(o), device_id_type=MESH)
        return carry

    lax.fori_loop(1, n, greet, 0)
    pl.semaphore_wait(barrier, n - 1)

    def copy(o):
        return pltpu.make_async_remote_copy(
            src_ref=sums_ref,
            dst_ref=held.at[me],
            send_sem=send_sem.at[o],
            recv_sem=recv_sem.at[o],
            device_id=place(o),
            device_id_type=MESH,
        )

    def start(o, carry):
        copy(o).start()
        return carry

    lax.fori_loop(1, n, start, 0)
    held[me] = sums_ref[...]

    def finish(o, carry):
        copy(o).wait()
        return carry

    lax.fori_loop(1, n, finish, 0)
    total = jnp.sum(jnp.sum(held[...], axis=0), axis=1, keepdims=True)
    for c in range(2):
        old, curve, cross, square = [total[4 * c + s : 4 * c + s + 1] for s in range(4)]
        step = old / curve
        new = jnp.maximum(old - 2.0 * step * cross + step * step * square, 0.0)
        beta = new / (old + TINY)
        s_out[c : c + 1, :] = jnp.broadcast_to(step, (1, LANES))
        rows = min(8, res_ref.shape[1])

        def strip(t, carry):
            at = pl.ds(pl.multiple_of(t * rows, rows), rows)
            r = res_ref[c, at, :] - step * image_ref[c, at, :]
            r_out[c, at, :] = r
            d_out[c, at, :] = r + beta * dir_ref[c, at, :]
            return carry

        lax.fori_loop(0, res_ref.shape[1] // rows, strip, 0)


def params(**more):
    return pltpu.CompilerParams(vmem_limit_bytes=GRANT, **more)


def pair_body(n_row, n_sub, residual_in, direction, weights, noise_var):
    _, rows, grid_len = direction.shape
    embed = 2 * grid_len
    low, half = embed // LANES, grid_len // LANES
    n = n_row * n_sub
    per = LANES // n
    f32 = jnp.float32
    vmem = pl.BlockSpec(memory_space=pltpu.VMEM)
    chunks = CHUNKS
    per_chunk = low // chunks
    aligned = (2 * per) % 8 == 0
    groups = n if aligned else 1

    slots, seconds = np.arange(LANES), np.arange(low)
    turn_cos, turn_sin = unit(slots[:, None] * seconds[None, :], embed, -1.0)
    wide_cos, wide_sin = jnp.asarray(turn_cos, f32), jnp.asarray(turn_sin, f32)
    tall_cos, tall_sin = jnp.asarray(turn_cos.T, f32), jnp.asarray(turn_sin.T, f32)
    fwd = complex_block(*unit(slots[:, None] * slots[None, :], LANES, -1.0))
    inv = complex_block(*unit(slots[:, None] * slots[None, :], LANES, 1.0))
    scale = 1.0 / (embed * embed)
    col_fwd = halves(fwd.reshape(2 * LANES, 2 * LANES))
    col_inv = halves(inv.reshape(2 * LANES, 2 * LANES) * scale)
    row_fwd = halves(
        fwd.reshape(2, LANES, 2, n, per).transpose(3, 2, 4, 0, 1).reshape(2 * LANES, 2 * LANES)
    )
    row_inv = halves(
        inv.reshape(2, n, per, 2, LANES).transpose(3, 4, 1, 0, 2).reshape(2 * LANES, 2 * LANES)
    )

    spread = pl.pallas_call(
        functools.partial(row_kernel, low, groups),
        out_shape=[jax.ShapeDtypeStruct((groups, per_chunk, 2 * LANES // groups, rows), f32)] * chunks,
        in_specs=[vmem] * 4,
        out_specs=[vmem] * chunks,
        scratch_shapes=[pltpu.VMEM((low, 2, LANES, rows), f32), pltpu.VMEM((half, 2, LANES, rows), f32)],
        compiler_params=params(),
        name="rows_out",
    )(direction, row_fwd, wide_cos, wide_sin)

    def swap(x):
        return lax.all_to_all(x, ("row", "sub"), split_axis=0, concat_axis=0, tiled=True)

    back = []
    for i, x in enumerate(spread):
        if not aligned:
            x = x.reshape(per_chunk, n, 2 * per, rows).transpose(1, 0, 2, 3)
        x = swap(x)
        if rows != LANES:
            x = x.reshape(half, LANES // rows, per_chunk, 2 * per, rows).transpose(0, 2, 3, 1, 4)
            x = x.reshape(half, per_chunk, 2 * per, LANES)
        x = pl.pallas_call(
            functools.partial(column_kernel, low, per),
            out_shape=jax.ShapeDtypeStruct((half, per_chunk, 2 * per, LANES), f32),
            in_specs=[vmem] * 6,
            out_specs=vmem,
            scratch_shapes=[pltpu.VMEM((low, per_chunk, per, 2 * LANES), f32)],
            compiler_params=params(),
            name=f"columns{i}",
        )(x, weights[:, i * per_chunk : (i + 1) * per_chunk], col_fwd, col_inv, tall_cos, tall_sin)
        if rows != LANES:
            x = x.reshape(half, per_chunk, 2 * per, LANES // rows, rows).transpose(0, 3, 1, 2, 4)
            x = x.reshape(n, per_chunk, 2 * per, rows)
        x = swap(x)
        if not aligned:
            x = x.transpose(1, 0, 2, 3).reshape(1, per_chunk, 2 * LANES, rows)
        back.append(x)

    image, sums = pl.pallas_call(
        functools.partial(image_kernel, low, groups, chunks),
        out_shape=[jax.ShapeDtypeStruct(direction.shape, f32), jax.ShapeDtypeStruct((8, LANES), f32)],
        in_specs=[vmem] * (chunks + 2) + [pl.BlockSpec(memory_space=pltpu.SMEM)] + [vmem] * 3,
        out_specs=[vmem] * 2,
        scratch_shapes=[pltpu.VMEM((low, 2, LANES, rows), f32), pltpu.VMEM((half, 2, LANES, rows), f32)],
        compiler_params=params(),
        name="rows_back",
    )(*back, direction, residual_in, noise_var, row_inv, wide_cos, wide_sin)

    residual_out, direction_out, steps = pl.pallas_call(
        functools.partial(update_kernel, n_row, n_sub),
        out_shape=[
            jax.ShapeDtypeStruct(direction.shape, f32),
            jax.ShapeDtypeStruct(direction.shape, f32),
            jax.ShapeDtypeStruct((2, LANES), f32),
        ],
        in_specs=[vmem] * 4,
        out_specs=[vmem] * 3,
        scratch_shapes=[
            pltpu.VMEM((n, 8, LANES), f32),
            pltpu.SemaphoreType.DMA((n,)),
            pltpu.SemaphoreType.DMA((n,)),
        ],
        compiler_params=params(collective_id=0, has_side_effects=True),
        name="update",
    )(sums, image, direction, residual_in)
    return residual_out, direction_out, steps[:, 0]


def solution(mesh):
    n_row, n_sub = mesh.shape["row"], mesh.shape["sub"]

    def body(residual_in, direction, spectrum, noise_var):
        embed = spectrum.shape[0]
        low = embed // LANES
        per = LANES // (n_row * n_sub)
        weights = spectrum.reshape(LANES, low, per, low).transpose(1, 3, 2, 0)
        return pair_body(n_row, n_sub, residual_in, direction, weights, noise_var)

    placed = P("grp", ("row", "sub"), None)
    return jax.shard_map(
        body,
        mesh=mesh,
        in_specs=(placed, placed, P("grp", ("row", "sub")), P("grp")),
        out_specs=(placed, placed, P("grp")),
        check_vma=False,
    )
```

profile of v0, /device:TPU:0, one launch (start us, length us, event | category | flops | bytes accessed | tf_op | source)
XLA Modules:
  0.0 322.7 jit_solution(9156259643931043089)
XLA Ops:
  0.6 15.0 %rows_out.1 = (f32[16,8,16,128]{3,2,1,0:T(8,128)}, f32[16,8,16,128]{3,2,1,0:T(8,128)}, f32[16,8,16,128]{3,2,1,0:T(8,128)}, f32[16,8,16,128]{3,2,1,0:T(8,128)}) custom-call(f32[2,128,2048]{2,1,0:T(8,128)} %dir_ref.3, bf16[2,256,256]{2,1,0:T(8,128)(2,1)} %constant.22.clone.table_ref, f32[128,32]{1,0:T(8,128)} %constant.16.clone.cos_ref.refs_8_, ...), custom_call_target="tpu_custom_call" | custom-call | tf_op jit(solution)/shard_map/rows_out/pallas_call | solution.py:312
  15.6 34.5 %all_to_all.40.x_ref = f32[16,8,16,128]{3,2,1,0:T(8,128)} all-to-all(f32[16,8,16,128]{3,2,1,0:T(8,128)} %get-tuple-element.12), channel_id=1, replica_groups=mesh['grp'=2,'row'=4,'sub'=4] {'row','sub'}, dimensions={0} | all-to-all | bytes 2097152 | tf_op jit(solution)/shard_map/all_to_all | solution.py:323
  50.1 30.2 %all_to_all.41.x_ref = f32[16,8,16,128]{3,2,1,0:T(8,128)} all-to-all(f32[16,8,16,128]{3,2,1,0:T(8,128)S(1)} %copy-done.7), channel_id=1, replica_groups=mesh['grp'=2,'row'=4,'sub'=4] {'row','sub'}, dimensions={0} | all-to-all | bytes 2097152 | tf_op jit(solution)/shard_map/all_to_all | solution.py:323
  80.2 30.2 %all_to_all.42.x_ref = f32[16,8,16,128]{3,2,1,0:T(8,128)} all-to-all(f32[16,8,16,128]{3,2,1,0:T(8,128)S(1)} %copy-done.6), channel_id=1, replica_groups=mesh['grp'=2,'row'=4,'sub'=4] {'row','sub'}, dimensions={0} | all-to-all | bytes 2097152 | tf_op jit(solution)/shard_map/all_to_all | solution.py:323
  110.4 3.7 %all-to-all-start.6 = ((f32[16,8,16,128]{3,2,1,0:T(8,128)}), f32[16,8,16,128]{3,2,1,0:T(8,128)S(1)}, u32[]{:S(2)}, u32[]{:S(2)}) async-start(f32[16,8,16,128]{3,2,1,0:T(8,128)} %get-tuple-element.15), calls=%async_computation.6 | async-start | bytes 2097152 | tf_op jit(solution)/shard_map/all_to_all | solution.py:323
  114.0 10.9 %reshape.9 = f32[128,32,8,32]{3,2,1,0:T(8,128)} reshape(f32[4096,256]{1,0:T(8,128)} %param.14) | data formatting | bytes 8388608 | tf_op jit(solution)/shard_map/reshape | solution.py:387
  124.9 13.9 %copy.15 = f32[128,32,8,32]{0,2,3,1:T(8,128)} copy(f32[128,32,8,32]{3,2,1,0:T(8,128)} %reshape.9) | data formatting | bytes 8388608 | tf_op jit(solution)/shard_map/reshape | solution.py:387
  138.8 4.4 %fusion = (f32[32,8,8,128]{3,2,1,0:T(8,128)}, f32[32,8,8,128]{3,2,1,0:T(8,128)}, f32[32,8,8,128]{3,2,1,0:T(8,128)}, f32[32,8,8,128]{3,2,1,0:T(8,128)}) fusion(f32[32,32,8,128]{3,2,1,0:T(8,128)} %bitcast.1), kind=kLoop, calls=%fused_computation.1 | loop fusion | bytes 8388608 | tf_op jit(solution)/shard_map/slice | solution.py:341
  143.2 17.8 %columns0.1 = f32[16,8,16,128]{3,2,1,0:T(8,128)} custom-call(f32[16,8,16,128]{3,2,1,0:T(8,128)} %all_to_all.40.x_ref, f32[32,8,8,128]{3,2,1,0:T(8,128)} %get-tuple-element.24.w_ref, bf16[2,256,256]{2,1,0:T(8,128)(2,1)} %constant.20.clone.fwd_ref, bf16[2,256,256]{2,1,0:T(8,128)(2,1)} %constant.21.clone.inv_ref, f32[32,128]{1,0:T(8,128)} %constant.18.clone.cos_ref, ...), custom_call_target="tpu_custom_call" | custom-call | tf_op jit(solution)/shard_map/columns0/pallas_call | solution.py:333
  161.1 5.9 %all-to-all-start.1 = ((f32[16,8,16,128]{3,2,1,0:T(8,128)}), f32[16,8,16,128]{3,2,1,0:T(8,128)S(1)}, u32[]{:S(2)}, u32[]{:S(2)}) async-start(f32[16,8,16,128]{3,2,1,0:T(8,128)} %columns0.1), calls=%async_computation.1 | async-start | bytes 2097152 | tf_op jit(solution)/shard_map/all_to_all | solution.py:323
  167.0 17.9 %columns1.1 = f32[16,8,16,128]{3,2,1,0:T(8,128)} custom-call(f32[16,8,16,128]{3,2,1,0:T(8,128)} %all_to_all.41.x_ref, f32[32,8,8,128]{3,2,1,0:T(8,128)} %get-tuple-element.23.w_ref, bf16[2,256,256]{2,1,0:T(8,128)(2,1)} %constant.20.clone.fwd_ref, bf16[2,256,256]{2,1,0:T(8,128)(2,1)} %constant.21.clone.inv_ref, f32[32,128]{1,0:T(8,128)} %constant.18.clone.cos_ref, ...), custom_call_target="tpu_custom_call" | custom-call | tf_op jit(solution)/shard_map/columns1/pallas_call | solution.py:333
  184.9 9.0 %all-to-all-done.1.refs_0_ = f32[16,8,16,128]{3,2,1,0:T(8,128)S(1)} async-done(((f32[16,8,16,128]{3,2,1,0:T(8,128)}), f32[16,8,16,128]{3,2,1,0:T(8,128)S(1)}, u32[]{:S(2)}, u32[]{:S(2)}) %all-to-all-start.1) | async-done | bytes 1048608 | tf_op jit(solution)/shard_map/all_to_all | solution.py:323
  193.9 3.7 %all-to-all-start.3 = ((f32[16,8,16,128]{3,2,1,0:T(8,128)}), f32[16,8,16,128]{3,2,1,0:T(8,128)S(1)}, u32[]{:S(2)}, u32[]{:S(2)}) async-start(f32[16,8,16,128]{3,2,1,0:T(8,128)} %columns1.1), calls=%async_computation.3 | async-start | bytes 2097152 | tf_op jit(solution)/shard_map/all_to_all | solution.py:323
  197.5 17.9 %columns2.1 = f32[16,8,16,128]{3,2,1,0:T(8,128)} custom-call(f32[16,8,16,128]{3,2,1,0:T(8,128)} %all_to_all.42.x_ref, f32[32,8,8,128]{3,2,1,0:T(8,128)} %get-tuple-element.22.w_ref, bf16[2,256,256]{2,1,0:T(8,128)(2,1)} %constant.20.clone.fwd_ref, bf16[2,256,256]{2,1,0:T(8,128)(2,1)} %constant.21.clone.inv_ref, f32[32,128]{1,0:T(8,128)} %constant.18.clone.cos_ref, ...), custom_call_target="tpu_custom_call" | custom-call | tf_op jit(solution)/shard_map/columns2/pallas_call | solution.py:333
  215.4 9.0 %all-to-all-done.3.refs_1_ = f32[16,8,16,128]{3,2,1,0:T(8,128)S(1)} async-done(((f32[16,8,16,128]{3,2,1,0:T(8,128)}), f32[16,8,16,128]{3,2,1,0:T(8,128)S(1)}, u32[]{:S(2)}, u32[]{:S(2)}) %all-to-all-start.3) | async-done | bytes 1048608 | tf_op jit(solution)/shard_map/all_to_all | solution.py:323
  224.4 3.7 %all-to-all-start.5 = ((f32[16,8,16,128]{3,2,1,0:T(8,128)}), f32[16,8,16,128]{3,2,1,0:T(8,128)S(1)}, u32[]{:S(2)}, u32[]{:S(2)}) async-start(f32[16,8,16,128]{3,2,1,0:T(8,128)} %columns2.1), calls=%async_computation.5 | async-start | bytes 2097152 | tf_op jit(solution)/shard_map/all_to_all | solution.py:323
  228.0 17.9 %columns3.1 = f32[16,8,16,128]{3,2,1,0:T(8,128)} custom-call(f32[16,8,16,128]{3,2,1,0:T(8,128)} %copy-done.1, f32[32,8,8,128]{3,2,1,0:T(8,128)} %get-tuple-element.21.w_ref, bf16[2,256,256]{2,1,0:T(8,128)(2,1)} %constant.20.clone.fwd_ref, bf16[2,256,256]{2,1,0:T(8,128)(2,1)} %constant.21.clone.inv_ref, f32[32,128]{1,0:T(8,128)} %constant.18.clone.cos_ref, ...), custom_call_target="tpu_custom_call" | custom-call | tf_op jit(solution)/shard_map/columns3/pallas_call | solution.py:333
  245.9 8.9 %all-to-all-done.5.refs_2_ = f32[16,8,16,128]{3,2,1,0:T(8,128)S(1)} async-done(((f32[16,8,16,128]{3,2,1,0:T(8,128)}), f32[16,8,16,128]{3,2,1,0:T(8,128)S(1)}, u32[]{:S(2)}, u32[]{:S(2)}) %all-to-all-start.5) | async-done | bytes 1048608 | tf_op jit(solution)/shard_map/all_to_all | solution.py:323
  254.8 3.7 %all-to-all-start.7 = ((f32[16,8,16,128]{3,2,1,0:T(8,128)}), f32[16,8,16,128]{3,2,1,0:T(8,128)S(1)}, u32[]{:S(2)}, u32[]{:S(2)}) async-start(f32[16,8,16,128]{3,2,1,0:T(8,128)} %columns3.1), calls=%async_computation.7 | async-start | bytes 2097152 | tf_op jit(solution)/shard_map/all_to_all | solution.py:323
  259.1 26.2 %all-to-all-done.7.refs_3_ = f32[16,8,16,128]{3,2,1,0:T(8,128)S(1)} async-done(((f32[16,8,16,128]{3,2,1,0:T(8,128)}), f32[16,8,16,128]{3,2,1,0:T(8,128)S(1)}, u32[]{:S(2)}, u32[]{:S(2)}) %all-to-all-start.7) | async-done | bytes 1048608 | tf_op jit(solution)/shard_map/all_to_all | solution.py:323
  286.3 17.2 %rows_back.1 = (f32[2,128,2048]{2,1,0:T(8,128)}, f32[8,128]{1,0:T(8,128)}) custom-call(f32[16,8,16,128]{3,2,1,0:T(8,128)} %copy-done, f32[16,8,16,128]{3,2,1,0:T(8,128)} %copy-done.2, f32[16,8,16,128]{3,2,1,0:T(8,128)} %copy-done.3, f32[16,8,16,128]{3,2,1,0:T(8,128)} %copy-done.4, f32[2,128,2048]{2,1,0:T(8,128)} %dir_ref.3, f32[2,128,2048]{2,1,0:T(8,128)} %res_ref.1, ...), custom_call_target="tpu_custom_call" | custom-call | tf_op jit(solution)/shard_map/rows_back/pallas_call | solution.py:350
  303.5 13.3 %update.1 = (f32[2,128,2048]{2,1,0:T(8,128)}, f32[2,128,2048]{2,1,0:T(8,128)}, f32[2,128]{1,0:T(2,128)}) custom-call(f32[8,128]{1,0:T(8,128)} %get-tuple-element.16.sums_ref, f32[2,128,2048]{2,1,0:T(8,128)} %get-tuple-element.17.image_ref, f32[2,128,2048]{2,1,0:T(8,128)} %dir_ref.3, f32[2,128,2048]{2,1,0:T(8,128)} %res_ref.1), custom_call_target="tpu_custom_call" | custom-call | tf_op jit(solution)/shard_map/update/pallas_call | solution.py:360
  318.1 3.3 %copy.19 = f32[2,128,2048]{2,1,0:T(8,128)} copy(f32[2,128,2048]{2,1,0:T(8,128)} %get-tuple-element.28) | data formatting | bytes 4194304
  321.4 1.3 copy.20
  (18 shorter events, 2.3 us)
Async XLA Ops:
  15.6 34.5 %copy-start.7 = (f32[16,8,16,128]{3,2,1,0:T(8,128)S(1)}, f32[16,8,16,128]{3,2,1,0:T(8,128)}, u32[]{:S(2)}) copy-start(f32[16,8,16,128]{3,2,1,0:T(8,128)} %get-tuple-element.13) | copy-start | bytes 3145732
  15.6 64.6 %copy-start.6 = (f32[16,8,16,128]{3,2,1,0:T(8,128)S(1)}, f32[16,8,16,128]{3,2,1,0:T(8,128)}, u32[]{:S(2)}) copy-start(f32[16,8,16,128]{3,2,1,0:T(8,128)} %get-tuple-element.14) | copy-start | bytes 3145732
  110.4 50.7 %all-to-all-start.6 = ((f32[16,8,16,128]{3,2,1,0:T(8,128)}), f32[16,8,16,128]{3,2,1,0:T(8,128)S(1)}, u32[]{:S(2)}, u32[]{:S(2)}) async-start(f32[16,8,16,128]{3,2,1,0:T(8,128)} %get-tuple-element.15), calls=%async_computation.6 | async-start | bytes 2097152 | tf_op jit(solution)/shard_map/all_to_all | solution.py:323
  161.1 23.8 %copy-start.1 = (f32[16,8,16,128]{3,2,1,0:T(8,128)}, f32[16,8,16,128]{3,2,1,0:T(8,128)S(1)}, u32[]{:S(2)}) copy-start(f32[16,8,16,128]{3,2,1,0:T(8,128)S(1)} %all-to-all-done.6.x_ref) | copy-start | bytes 3145732
  161.1 32.8 %all-to-all-start.1 = ((f32[16,8,16,128]{3,2,1,0:T(8,128)}), f32[16,8,16,128]{3,2,1,0:T(8,128)S(1)}, u32[]{:S(2)}, u32[]{:S(2)}) async-start(f32[16,8,16,128]{3,2,1,0:T(8,128)} %columns0.1), calls=%async_computation.1 | async-start | bytes 2097152 | tf_op jit(solution)/shard_map/all_to_all | solution.py:323
  193.9 21.5 %copy-start = (f32[16,8,16,128]{3,2,1,0:T(8,128)}, f32[16,8,16,128]{3,2,1,0:T(8,128)S(1)}, u32[]{:S(2)}) copy-start(f32[16,8,16,128]{3,2,1,0:T(8,128)S(1)} %all-to-all-done.1.refs_0_) | copy-start | bytes 3145732
  193.9 30.5 %all-to-all-start.3 = ((f32[16,8,16,128]{3,2,1,0:T(8,128)}), f32[16,8,16,128]{3,2,1,0:T(8,128)S(1)}, u32[]{:S(2)}, u32[]{:S(2)}) async-start(f32[16,8,16,128]{3,2,1,0:T(8,128)} %columns1.1), calls=%async_computation.3 | async-start | bytes 2097152 | tf_op jit(solution)/shard_map/all_to_all | solution.py:323
  224.3 21.5 %copy-start.2 = (f32[16,8,16,128]{3,2,1,0:T(8,128)}, f32[16,8,16,128]{3,2,1,0:T(8,128)S(1)}, u32[]{:S(2)}) copy-start(f32[16,8,16,128]{3,2,1,0:T(8,128)S(1)} %all-to-all-done.3.refs_1_) | copy-start | bytes 3145732
  224.4 30.5 %all-to-all-start.5 = ((f32[16,8,16,128]{3,2,1,0:T(8,128)}), f32[16,8,16,128]{3,2,1,0:T(8,128)S(1)}, u32[]{:S(2)}, u32[]{:S(2)}) async-start(f32[16,8,16,128]{3,2,1,0:T(8,128)} %columns2.1), calls=%async_computation.5 | async-start | bytes 2097152 | tf_op jit(solution)/shard_map/all_to_all | solution.py:323
  254.8 30.5 %copy-start.3 = (f32[16,8,16,128]{3,2,1,0:T(8,128)}, f32[16,8,16,128]{3,2,1,0:T(8,128)S(1)}, u32[]{:S(2)}) copy-start(f32[16,8,16,128]{3,2,1,0:T(8,128)S(1)} %all-to-all-done.5.refs_2_) | copy-start | bytes 3145732
  254.8 30.5 %all-to-all-start.7 = ((f32[16,8,16,128]{3,2,1,0:T(8,128)}), f32[16,8,16,128]{3,2,1,0:T(8,128)S(1)}, u32[]{:S(2)}, u32[]{:S(2)}) async-start(f32[16,8,16,128]{3,2,1,0:T(8,128)} %columns3.1), calls=%async_computation.7 | async-start | bytes 2097152 | tf_op jit(solution)/shard_map/all_to_all | solution.py:323
  285.3 1.0 copy-start.4
  318.1 3.3 %copy-start.5 = (f32[2,128,2048]{2,1,0:T(8,128)S(1)}, f32[2,128,2048]{2,1,0:T(8,128)}, u32[]{:S(2)}) copy-start(f32[2,128,2048]{2,1,0:T(8,128)} %get-tuple-element.29) | copy-start | bytes 6291460
where the time goes:
time: 324 us; the launch traced here: 323 us
  Pallas kernels  117 us (36%)
  blocking collectives  94.8 us (29%)
  waiting for transfers between devices  53 us (16%)
  local copies, waits for them, and re-layouts  36.1 us (11%)
  starting transfers between devices  20.6 us (6%)
    all_to_all x3, blocking collectives, swap(): lax.all_to_all(x, ('row', 'sub'), split_axis=0, concat_axis=0, tiled=True)  94.8 us
    pallas_call x4, Pallas kernels, pair_body(): pl.pallas_call(functools.partial(column_kernel, low, per), out_shape=jax....  71.5 us
    all_to_all x5, waiting for transfers between devices, swap(): lax.all_to_all(x, ('row', 'sub'), split_axis=0, concat_axis=0, tiled=True)  53 us
    reshape x2, local copies, waits for them, and re-layouts, body(): weights = spectrum.reshape(LANES, low, per, low).transpose(1, 3, 2, 0)  24.8 us
    all_to_all x5, starting transfers between devices, swap(): lax.all_to_all(x, ('row', 'sub'), split_axis=0, concat_axis=0, tiled=True)  20.6 us
    pallas_call x1, Pallas kernels, pair_body(): pl.pallas_call(functools.partial(image_kernel, low, groups, chunks), out_...  17.2 us
    pallas_call x1, Pallas kernels, pair_body(): pl.pallas_call(functools.partial(row_kernel, low, groups), out_shape=[jax...  15 us
    pallas_call x1, Pallas kernels, pair_body(): pl.pallas_call(functools.partial(update_kernel, n_row, n_sub), out_shape=...  13.3 us
  transfers between devices with their start and end apart: 5, of which 4 were waited for; matrix products, arithmetic and copies ran while one was open for 9% of the time, Pallas kernels for 22%

commit v1 on v0

--- a/solution.py
+++ b/solution.py
@@ -280,19 +280,8 @@
     return pltpu.CompilerParams(vmem_limit_bytes=GRANT, **more)
 
 
-def pair_body(n_row, n_sub, residual_in, direction, weights, noise_var):
-    _, rows, grid_len = direction.shape
-    embed = 2 * grid_len
-    low, half = embed // LANES, grid_len // LANES
-    n = n_row * n_sub
-    per = LANES // n
-    f32 = jnp.float32
-    vmem = pl.BlockSpec(memory_space=pltpu.VMEM)
-    chunks = CHUNKS
-    per_chunk = low // chunks
-    aligned = (2 * per) % 8 == 0
-    groups = n if aligned else 1
-
+def make_tables(embed, n, per):
+    low, f32 = embed // LANES, jnp.float32
     slots, seconds = np.arange(LANES), np.arange(low)
     turn_cos, turn_sin = unit(slots[:, None] * seconds[None, :], embed, -1.0)
     wide_cos, wide_sin = jnp.asarray(turn_cos, f32), jnp.asarray(turn_sin, f32)
@@ -308,6 +297,23 @@
     row_inv = halves(
         inv.reshape(2, n, per, 2, LANES).transpose(3, 4, 1, 0, 2).reshape(2 * LANES, 2 * LANES)
     )
+    return row_fwd, row_inv, col_fwd, col_inv, wide_cos, wide_sin, tall_cos, tall_sin
+
+
+def pair_body(n_row, n_sub, residual_in, direction, weights, noise_var):
+    _, rows, grid_len = direction.shape
+    embed = 2 * grid_len
+    low, half = embed // LANES, grid_len // LANES
+    n = n_row * n_sub
+    per = LANES // n
+    f32 = jnp.float32
+    vmem = pl.BlockSpec(memory_space=pltpu.VMEM)
+    chunks = CHUNKS
+    per_chunk = low // chunks
+    aligned = (2 * per) % 8 == 0
+    groups = n if aligned else 1
+
+    row_fwd, row_inv, col_fwd, col_inv, wide_cos, wide_sin, tall_cos, tall_sin = make_tables(embed, n, per)
 
     spread = pl.pallas_call(
         functools.partial(row_kernel, low, groups),
@@ -377,6 +383,254 @@
     return residual_out, direction_out, steps[:, 0]
 
 
+def fused_kernel(
+    low, chunks, n_row, n_sub,
+    dir_ref, res_hbm, spec_hbm, noise_ref, row_fwd, row_inv, col_fwd, col_inv,
+    wide_cos, wide_sin, tall_cos, tall_sin,
+    r_out, d_out, s_out,
+    res_ref, spec_ref, weights, work, turned, cols, send, recv, back_send, back_recv, held, sums_ref,
+    load_sem, send_sem, recv_sem, back_send_sem, back_recv_sem, sum_send_sem, sum_recv_sem,
+):
+    n = n_row * n_sub
+    half = low // 2
+    count = low // chunks
+    per = LANES // n
+    size = 2 * per
+    me = lax.axis_index("row") * n_sub + lax.axis_index("sub")
+
+    def place(o):
+        peer = lax.rem(me + o, n)
+        return peer, {"row": peer // n_sub, "sub": lax.rem(peer, n_sub)}
+
+    def loop(first, last, step):
+        def run(i, carry):
+            step(i)
+            return carry
+
+        lax.fori_loop(first, last, run, 0)
+
+    barrier = pltpu.get_barrier_semaphore()
+    loop(
+        1, n,
+        lambda o: pl.semaphore_signal(barrier, inc=1, device_id=place(o)[1], device_id_type=MESH),
+    )
+    load_res = pltpu.make_async_copy(res_hbm, res_ref, load_sem.at[0])
+    load_spec = [
+        pltpu.make_async_copy(spec_hbm.at[:, pl.ds(s * LANES, LANES)], spec_ref.at[s], load_sem.at[s + 1])
+        for s in range(spec_ref.shape[0])
+    ]
+    for load in load_spec:
+        load.start()
+    load_res.start()
+
+    def exchange(i, o, src, dst, s_sem, r_sem):
+        peer, device = place(o)
+        return pltpu.make_async_remote_copy(
+            src_ref=src.at[i, peer],
+            dst_ref=dst.at[i, me],
+            send_sem=s_sem.at[i, o],
+            recv_sem=r_sem.at[i, o],
+            device_id=device,
+            device_id_type=MESH,
+        )
+
+    def ahead(i, o):
+        return exchange(i, o, send, recv, send_sem, recv_sem)
+
+    def home(i, o):
+        return exchange(i, o, back_send, back_recv, back_send_sem, back_recv_sem)
+
+    for c in range(2):
+        for a in range(half):
+            turned[a, c] = dir_ref[c, :, a * LANES : (a + 1) * LANES].T
+
+    def spread_rows(t):
+        at = pl.ds(pl.multiple_of(t * 8, 8), 8)
+        xs = [(turned[a, 0, at, :], turned[a, 1, at, :]) for a in range(half)]
+        cos_rows, sin_rows = wide_cos[at, :], wide_sin[at, :]
+        for m, (re, im) in enumerate(padded_forward(xs)):
+            re, im = rotate(re, im, cos_rows[:, m : m + 1], sin_rows[:, m : m + 1])
+            work[m, 0, at, :] = re
+            work[m, 1, at, :] = im
+
+    loop(0, LANES // 8, spread_rows)
+
+    def send_chunk(i):
+        def column(m):
+            got = dot_left(row_fwd, work[i * count + m].reshape(2 * LANES, LANES))
+            for j in range(n):
+                send[i, j, m] = got[j * size : (j + 1) * size]
+
+        loop(0, count, column)
+        recv[i, me] = send[i, me]
+        loop(1, n, lambda o: ahead(i, o).start())
+
+    for i in range(chunks):
+        if i == 0:
+            pl.semaphore_wait(barrier, n - 1)
+        send_chunk(i)
+
+    for load in load_spec:
+        load.wait()
+
+    def turn_spectrum(k):
+        for s in range(spec_ref.shape[0]):
+            part = spec_ref[s, pl.ds(k, LANES, stride=low), :]
+            weights[k, s * LANES : (s + 1) * LANES, :] = part.T
+
+    loop(0, low, turn_spectrum)
+
+    def column_chunk(i):
+        loop(1, n, lambda o: ahead(i, o).wait_recv())
+
+        def spread(m):
+            xs = [(recv[i, a, m, :per], recv[i, a, m, per:]) for a in range(half)]
+            for k, (re, im) in enumerate(padded_forward(xs)):
+                re, im = rotate(re, im, tall_cos[k : k + 1, :], tall_sin[k : k + 1, :])
+                cols[k, m, :, :LANES] = re
+                cols[k, m, :, LANES:] = im
+
+        loop(0, count, spread)
+
+        def filtered(k):
+            spectral = dot_right(cols[k].reshape(count * per, 2 * LANES), col_fwd)
+            scale = jnp.concatenate(
+                [weights[k, pl.ds(i * count + m, per, stride=low), :] for m in range(count)], axis=0
+            )
+            spectral = spectral * jnp.concatenate([scale, scale], axis=1)
+            got = dot_right(spectral, col_inv)
+            cos_row, sin_row = tall_cos[pl.ds(k, 1), :], tall_sin[pl.ds(k, 1), :]
+            re, im = rotate(got[:, :LANES], got[:, LANES:], cos_row, -sin_row)
+            cols[k, :, :, :LANES] = re.reshape(count, per, LANES)
+            cols[k, :, :, LANES:] = im.reshape(count, per, LANES)
+
+        loop(0, low, filtered)
+
+        def gather(m):
+            zs = [(cols[k, m, :, :LANES], cols[k, m, :, LANES:]) for k in range(low)]
+            for a, (re, im) in enumerate(cut_inverse(zs)):
+                back_send[i, a, m, :per] = re
+                back_send[i, a, m, per:] = im
+
+        loop(0, count, gather)
+        back_recv[i, me] = back_send[i, me]
+        loop(1, n, lambda o: home(i, o).start())
+
+    for i in range(chunks):
+        column_chunk(i)
+
+    for i in range(chunks):
+        loop(1, n, lambda o: home(i, o).wait_recv())
+
+        def column(m):
+            got = dot_left(row_inv, jnp.concatenate([back_recv[i, j, m] for j in range(n)], axis=0))
+            work[i * count + m] = got.reshape(2, LANES, LANES)
+
+        loop(0, count, column)
+
+    def gather_rows(t):
+        at = pl.ds(pl.multiple_of(t * 8, 8), 8)
+        cos_rows, sin_rows = wide_cos[at, :], wide_sin[at, :]
+        zs = [
+            rotate(work[m, 0, at, :], work[m, 1, at, :], cos_rows[:, m : m + 1], -sin_rows[:, m : m + 1])
+            for m in range(low)
+        ]
+        for a, (re, im) in enumerate(cut_inverse(zs)):
+            turned[a, 0, at, :] = re
+            turned[a, 1, at, :] = im
+
+    loop(0, LANES // 8, gather_rows)
+    load_res.wait()
+    noise = noise_ref[0]
+    for c in range(2):
+        totals = [jnp.zeros((8, LANES), jnp.float32)] * 4
+        for a in range(half):
+            at = slice(a * LANES, (a + 1) * LANES)
+            d, r = dir_ref[c, :, at], res_ref[c, :, at]
+            image = turned[a, c].T + noise * d
+            d_out[c, :, at] = image
+            for s, term in enumerate((r * r, d * image, r * image, image * image)):
+                totals[s] = totals[s] + jnp.sum(term.reshape(LANES // 8, 8, LANES), axis=0)
+        for s in range(4):
+            sums_ref[4 * c + s : 4 * c + s + 1, :] = jnp.sum(totals[s], axis=0, keepdims=True)
+
+    def share(o):
+        return pltpu.make_async_remote_copy(
+            src_ref=sums_ref,
+            dst_ref=held.at[me],
+            send_sem=sum_send_sem.at[o],
+            recv_sem=sum_recv_sem.at[o],
+            device_id=place(o)[1],
+            device_id_type=MESH,
+        )
+
+    held[me] = sums_ref[...]
+    loop(1, n, lambda o: share(o).start())
+    for i in range(chunks):
+        loop(1, n, lambda o: ahead(i, o).wait_send())
+        loop(1, n, lambda o: home(i, o).wait_send())
+    loop(1, n, lambda o: share(o).wait())
+    total = jnp.sum(jnp.sum(held[...], axis=0), axis=1, keepdims=True)
+    for c in range(2):
+        old, curve, cross, square = [total[4 * c + s : 4 * c + s + 1] for s in range(4)]
+        step = old / curve
+        new = jnp.maximum(old - 2.0 * step * cross + step * step * square, 0.0)
+        beta = new / (old + TINY)
+        s_out[c : c + 1, :] = jnp.broadcast_to(step, (1, LANES))
+
+        def strip(t):
+            at = pl.ds(pl.multiple_of(t * 8, 8), 8)
+            r = res_ref[c, at, :] - step * d_out[c, at, :]
+            r_out[c, at, :] = r
+            d_out[c, at, :] = r + beta * dir_ref[c, at, :]
+
+        loop(0, LANES // 8, strip)
+
+
+def fused_body(n_row, n_sub, residual_in, direction, spectrum, noise_var):
+    _, rows, grid_len = direction.shape
+    embed = 2 * grid_len
+    low, half = embed // LANES, grid_len // LANES
+    n = n_row * n_sub
+    per = LANES // n
+    f32 = jnp.float32
+    vmem = pl.BlockSpec(memory_space=pltpu.VMEM)
+    away = pl.BlockSpec(memory_space=pl.ANY)
+    chunks = CHUNKS
+    count = low // chunks
+    tables = make_tables(embed, n, per)
+    block = pltpu.VMEM((chunks, n, count, 2 * per, LANES), f32)
+    flags = pltpu.SemaphoreType.DMA((chunks, n))
+    residual_out, direction_out, steps = pl.pallas_call(
+        functools.partial(fused_kernel, low, chunks, n_row, n_sub),
+        out_shape=[
+            jax.ShapeDtypeStruct(direction.shape, f32),
+            jax.ShapeDtypeStruct(direction.shape, f32),
+            jax.ShapeDtypeStruct((2, LANES), f32),
+        ],
+        in_specs=[vmem, away, away, pl.BlockSpec(memory_space=pltpu.SMEM)] + [vmem] * 8,
+        out_specs=[vmem] * 3,
+        scratch_shapes=[
+            pltpu.VMEM(direction.shape, f32),
+            pltpu.VMEM((spectrum.shape[1] // LANES, embed, LANES), f32),
+            pltpu.VMEM((low, spectrum.shape[1], LANES), f32),
+            pltpu.VMEM((low, 2, LANES, rows), f32),
+            pltpu.VMEM((half, 2, LANES, rows), f32),
+            pltpu.VMEM((low, count, per, 2 * LANES), f32),
+            block, block, block, block,
+            pltpu.VMEM((n, 8, LANES), f32),
+            pltpu.VMEM((8, LANES), f32),
+            pltpu.SemaphoreType.DMA((1 + spectrum.shape[1] // LANES,)),
+            flags, flags, flags, flags,
+            pltpu.SemaphoreType.DMA((n,)),
+            pltpu.SemaphoreType.DMA((n,)),
+        ],
+        compiler_params=params(collective_id=1, has_side_effects=True),
+        name="cg_step",
+    )(direction, residual_in, spectrum, noise_var, *tables)
+    return residual_out, direction_out, steps[:, 0]
+
+
 def solution(mesh):
     n_row, n_sub = mesh.shape["row"], mesh.shape["sub"]
 
@@ -384,6 +638,8 @@
         embed = spectrum.shape[0]
         low = embed // LANES
         per = LANES // (n_row * n_sub)
+        if direction.shape[1] == LANES and direction.shape[2] == LANES * n_row * n_sub and per % 8 == 0:
+            return fused_body(n_row, n_sub, residual_in, direction, spectrum, noise_var)
         weights = spectrum.reshape(LANES, low, per, low).transpose(1, 3, 2, 0)
         return pair_body(n_row, n_sub, residual_in, direction, weights, noise_var)
 

time: 324 us -> 215 us (0.66)
  blocking collectives: 94.8 us -> 0 us
  Pallas kernels: 117 us -> 208 us
  waiting for transfers between devices: 53 us -> 0 us
  local copies, waits for them, and re-layouts: 36.1 us -> 5.89 us
  starting transfers between devices: 20.6 us -> 0 us
    all_to_all x3 -> x0, blocking collectives: 94.8 us -> none  [swap(): lax.all_to_all(x, ('row', 'sub'), split_axis=0, concat_axis=0, tiled=True)]
    pallas_call x7 -> x1, Pallas kernels: 117 us -> 208 us  [fused_body(): pl.pallas_call(functools.partial(fused_kernel, low, chunks, n_row, n_sub)...]
    all_to_all x5 -> x0, waiting for transfers between devices: 53 us -> none  [swap(): lax.all_to_all(x, ('row', 'sub'), split_axis=0, concat_axis=0, tiled=True)]
    reshape x2 -> x0, local copies, waits for them, and re-layouts: 24.8 us -> none  [body(): weights = spectrum.reshape(LANES, low, per, low).transpose(1, 3, 2, 0)]
    all_to_all x5 -> x0, starting transfers between devices: 20.6 us -> none  [swap(): lax.all_to_all(x, ('row', 'sub'), split_axis=0, concat_axis=0, tiled=True)]
    slice x2 -> x1, local copies, waits for them, and re-layouts: 5.68 us -> 1.29 us  [fused_body(): return (residual_out, direction_out, steps[:, 0])]
  transfers between devices with their start and end apart: 5 -> 0, of which waited for: 4 -> 0; matrix products, arithmetic and copies ran while one was open for 9% -> 0% of each run, Pallas kernels for 22% -> 0%
where the time goes in v1:
time: 215 us
  Pallas kernels  208 us (97%)
  local copies, waits for them, and re-layouts  5.89 us (3%)
    pallas_call x1, Pallas kernels, fused_body(): pl.pallas_call(functools.partial(fused_kernel, low, chunks, n_row, n_sub)...  208 us
    unnamed x4, local copies, waits for them, and re-layouts  4.61 us

profile of v1, /device:TPU:0, one launch (start us, length us, event | category | flops | bytes accessed | tf_op | source)
XLA Modules:
  0.0 215.2 jit_solution(3315147192537206939)
XLA Ops:
  1.3 208.0 %cg_step.1 = (f32[2,128,2048]{2,1,0:T(8,128)}, f32[2,128,2048]{2,1,0:T(8,128)}, f32[2,128]{1,0:T(2,128)}) custom-call(f32[2,128,2048]{2,1,0:T(8,128)} %dir_ref.1, f32[2,128,2048]{2,1,0:T(8,128)} %res_hbm.1, f32[4096,256]{1,0:T(8,128)} %spec_hbm.1, f32[1]{0:T(128)S(6)} %copy.17.noise_ref, bf16[2,256,256]{2,1,0:T(8,128)(2,1)} %constant.22.clone.row_fwd, ...), custom_call_target="tpu_custom_call" | custom-call | tf_op jit(solution)/shard_map/cg_step/pallas_call | solution.py:604
  209.3 1.3 slice_reduce_fusion
  210.5 0.0 copy-start
  210.5 3.3 %copy.18 = f32[2,128,2048]{2,1,0:T(8,128)} copy(f32[2,128,2048]{2,1,0:T(8,128)} %get-tuple-element.12) | data formatting | bytes 4194304
  213.8 0.0 copy-done
  213.8 1.3 copy.19
Async XLA Ops:
  210.5 3.3 %copy-start = (f32[2,128,2048]{2,1,0:T(8,128)S(1)}, f32[2,128,2048]{2,1,0:T(8,128)}, u32[]{:S(2)}) copy-start(f32[2,128,2048]{2,1,0:T(8,128)} %get-tuple-element.13) | copy-start | bytes 6291460
